TPU v7x, 32 devices: a whole 2x2x4 slice. The times are simulated.
32 devices in a mesh: groups: 2 (over y), ctx: 4 (over z), heads: 4 (over x, core).
Axes of the slice: x: 2, y: 2, z: 4, core: 2. Of those that a mesh axis runs over, the one named last changes fastest.
Arguments:
- ssm_input: bfloat16 [2048, 8192], P(('groups', 'ctx'), 'heads'), parts along dimension 0, may hold values from -6 to 6
- decay_log: float32 [2048, 128], P(('groups', 'ctx'), 'heads'), parts along dimension 0
- state_write: bfloat16 [2048, 128], P(('groups', 'ctx')), parts along dimension 0, may hold values from -2 to 2
- state_read: bfloat16 [2048, 128], P(('groups', 'ctx')), parts along dimension 0, may hold values from -2 to 2
- skip_scale: float32 [128], P('heads'), may hold values from 0.5 to 3
- gate_input: bfloat16 [2048, 8192], P(('groups', 'ctx'), 'heads'), parts along dimension 0, may hold values from -6 to 6
- ssm_gain: float32 [8192], P('heads'), may hold values from 0.1 to 1.9
- out_weight: bfloat16 [8192, 4096], P('heads', 'ctx'), may hold values from -0.0625 to 0.0625
- residual_in: bfloat16 [2048, 4096], P(('groups', 'ctx'), 'heads'), parts along dimension 0, may hold values from -24 to 24
- moe_gain: float32 [4096], P('heads'), may hold values from 0.1 to 1.9
- down_latent: bfloat16 [4096, 1024], P('heads'), may hold values from -0.09375 to 0.09375
- expert_up: bfloat16 [8, 1024, 2688], P('ctx', None, 'heads'), may hold values from -0.1875 to 0.1875
- expert_down: bfloat16 [8, 2688, 1024], P('ctx', 'heads'), may hold values from -0.125 to 0.125
- up_latent: bfloat16 [1024, 4096], P(None, 'heads'), may hold values from -0.1875 to 0.1875
- expert_ids: int32 [2048, 22], P(('groups', 'ctx')), parts along dimension 0, may hold values from 0 to 511, as said below
- combine_fixed: int32 [2048, 22], P(('groups', 'ctx')), parts along dimension 0, may hold values from 1 to 65535
Outputs:
- layer_out: bfloat16 [2048, 4096], P(('groups', 'ctx'), 'heads'), parts along dimension 0
There are 2 independent parts, one for each index of `groups`. A program takes and returns all parts, laid end to end along the dimension named above; an argument that names none is the same for every part. Nothing has to cross between parts.
Inputs may be any that keep to these rules, and one draw needn't show every extreme that they name: `expert_ids`: each row names 22 different experts. No expert below 8 is named by more than 16 of the 256 tokens of one block, and in every block some expert below 8 is named by exactly 16 of them.
All inputs are finite; a program needn't handle non-finite values.
Results may differ from a plain program's by a relative error of at most 0.014.
Values may be sent and summed in bfloat16 or wider, within the bound.
A program may use at most 128 MiB of HBM per device.

v0:
```python
import jax
import jax.numpy as jnp
from jax import lax
from jax.sharding import PartitionSpec as P

D = 4096
GRP = 1024
LAT = 1024
CAP = 16


epsilon = 1e-05


def prefix(value, axis, combine, identity):
    length, here = (lax.axis_size(axis), lax.axis_index(axis))
    everything = jax.tree.map(
        lambda part, kind: lax.all_gather(part.astype(kind), axis),
        value,
        (jnp.bfloat16, jnp.bfloat16),
    )
    start = jax.tree.map(
        lambda part, zero: jnp.broadcast_to(jnp.asarray(zero, part.dtype), part.shape),
        value,
        identity,
    )

    def step(k, before):
        reached = k < here
        new = combine(
            before, jax.tree.map(lambda part, own: part[k].astype(own.dtype), everything, value)
        )
        return jax.tree.map(lambda a, b: jnp.where(reached, a, b), new, before)

    return lax.fori_loop(0, length, step, start)


def state_link(previous, current):
    return (previous[0] * current[0], current[0][:, None, None] * previous[1] + current[1])


def expert_apply(incoming, expert_up, expert_down):
    hidden = jnp.einsum("secl,elf->secf", incoming, expert_up, preferred_element_type=jnp.float32)
    hidden = (jnp.maximum(hidden, 0.0) ** 2).astype(jnp.bfloat16)
    return jnp.einsum("secf,efl->secl", hidden, expert_down, preferred_element_type=jnp.float32)


def local(
    ssm_input,
    decay_log,
    state_write,
    state_read,
    skip_scale,
    gate_input,
    ssm_gain,
    out_weight,
    residual_in,
    moe_gain,
    down_latent,
    expert_up,
    expert_down,
    up_latent,
    expert_ids,
    combine_fixed,
):
    row_count = ssm_input.shape[0]
    head_count = decay_log.shape[1]
    inputs = ssm_input.astype(jnp.float32).reshape(row_count, head_count, -1)
    writes = state_write.astype(jnp.float32)
    reads = state_read.astype(jnp.float32)
    cumulative = jnp.cumsum(decay_log, axis=0)
    causal = jnp.arange(row_count)[:, None] >= jnp.arange(row_count)[None, :]
    spread = jnp.where(causal[:, :, None], cumulative[:, None, :] - cumulative[None, :, :], 0.0)
    intersection = jnp.dot(state_read, state_write.T, preferred_element_type=jnp.float32)
    mixing = jnp.where(causal[:, :, None], jnp.exp(-spread), 0.0) * intersection[:, :, None]
    within = jnp.einsum("tsh,shp->thp", mixing, inputs, precision=lax.Precision.HIGHEST)
    tail_decay = jnp.exp(cumulative - cumulative[-1][None, :])
    local_state = jnp.einsum(
        "sn,sh,shp->hnp", writes, tail_decay, inputs, precision=lax.Precision.HIGHEST
    )
    local_decay = jnp.exp(-cumulative[-1])
    identity = (jnp.ones_like(local_decay), jnp.zeros_like(local_state))
    prior_decay, prior_state = prefix((local_decay, local_state), "ctx", state_link, identity)
    carried = (
        jnp.einsum("tn,hnp->thp", reads, prior_state, precision=lax.Precision.HIGHEST)
        * jnp.exp(-cumulative)[:, :, None]
    )
    mixed = within + carried + skip_scale[None, :, None] * inputs
    gated = mixed.reshape(row_count, -1) * jax.nn.silu(gate_input.astype(jnp.float32))
    grouped = gated.reshape(row_count, -1, GRP)
    group_rms = lax.rsqrt(jnp.mean(grouped * grouped, axis=2, keepdims=True) + epsilon)
    normed = ((grouped * group_rms).reshape(gated.shape) * ssm_gain).astype(jnp.bfloat16)
    partial_value = jnp.dot(
        normed,
        lax.all_gather(out_weight, "ctx", axis=1, tiled=True),
        preferred_element_type=jnp.float32,
    )
    mamba_out = lax.psum_scatter(
        partial_value.astype(jnp.bfloat16), "heads", scatter_dimension=1, tiled=True
    ).astype(jnp.float32)
    residual = residual_in.astype(jnp.float32) + mamba_out
    scaled = (residual * moe_gain).astype(jnp.bfloat16)
    latent_part = jnp.dot(scaled, down_latent, preferred_element_type=jnp.float32)
    squares = jnp.sum(residual * residual, axis=1)
    latent_sum, square_sum = (
        lax.psum(latent_part.astype(jnp.bfloat16), "heads").astype(jnp.float32),
        lax.psum(squares.astype(jnp.bfloat16), "heads").astype(jnp.float32),
    )
    inv_rms = lax.rsqrt(square_sum / D + epsilon)
    latent = (latent_sum * inv_rms[:, None]).astype(jnp.bfloat16)
    ctx_count = lax.axis_size("ctx")
    experts_here = expert_up.shape[0]
    wave_size = experts_here * ctx_count
    matches = expert_ids[:, :, None] == jnp.arange(wave_size)[None, None, :]
    chosen = jnp.any(matches, axis=1).astype(jnp.int32)
    weight_fixed = jnp.sum(jnp.where(matches, combine_fixed[:, :, None], 0), axis=1)
    slot_index = jnp.cumsum(chosen, axis=0) - 1
    placed = (chosen[:, :, None] == 1) & (slot_index[:, :, None] == jnp.arange(CAP)[None, None, :])
    route_weight = (weight_fixed.astype(jnp.float32) / 65536.0).astype(jnp.bfloat16)
    combine_table = jnp.where(placed, route_weight[:, :, None], jnp.zeros((), jnp.bfloat16))
    outgoing = jnp.einsum(
        "tk,tl->kl",
        placed.astype(jnp.bfloat16).reshape(row_count, wave_size * CAP),
        latent,
        preferred_element_type=jnp.float32,
    )
    outgoing = outgoing.astype(jnp.bfloat16).reshape(ctx_count, experts_here, CAP, LAT)
    incoming = lax.all_to_all(outgoing, "ctx", split_axis=0, concat_axis=0, tiled=True)
    expert_out = lax.psum(
        expert_apply(incoming, expert_up, expert_down).astype(jnp.bfloat16), "heads"
    )
    returned = lax.all_to_all(expert_out, "ctx", split_axis=0, concat_axis=0, tiled=True).reshape(
        wave_size * CAP, LAT
    )
    combined = jnp.einsum(
        "tk,kl->tl",
        combine_table.reshape(row_count, wave_size * CAP),
        returned,
        preferred_element_type=jnp.float32,
    )
    moe_out = jnp.dot(combined.astype(jnp.bfloat16), up_latent, preferred_element_type=jnp.float32)
    return (residual + moe_out).astype(jnp.bfloat16)


def solution(mesh):
    placed = (
        P(("groups", "ctx"), "heads"),
        P(("groups", "ctx"), "heads"),
        P(("groups", "ctx"), None),
        P(("groups", "ctx"), None),
        P("heads"),
        P(("groups", "ctx"), "heads"),
        P("heads"),
        P("heads", "ctx"),
        P(("groups", "ctx"), "heads"),
        P("heads"),
        P("heads", None),
        P("ctx", None, "heads"),
        P("ctx", "heads", None),
        P(None, "heads"),
        P(("groups", "ctx"), None),
        P(("groups", "ctx"), None),
    )
    return jax.shard_map(
        local, mesh=mesh, in_specs=placed, out_specs=P(("groups", "ctx"), "heads"), check_vma=False
    )
```

profile of v0, /device:TPU:1, one launch (start us, length us, event | category | flops | bytes accessed | tf_op | source)
XLA Modules:
  0.0 498.0 jit_solution(15376862244414403239)
XLA Ops:
  8.6 2.3 copy.76
  10.9 3.2 fusion.28
  15.1 10.0 %all-gather.1 = bf16[4,1,32]{2,1,0:T(2,128)(2,1)S(1)} all-gather(bf16[1,1,32]{2,1,0:T(2,128)(2,1)S(1)} %bitcast.123), channel_id=1, replica_groups=mesh['groups'=2,'ctx'=4,'heads'=4] {'ctx'}, dimensions={0}, use_global_device_ids=true | all-gather | bytes 320 | tf_op jit(solution)/shard_map/all_gather | solution.py:18
  26.0 35.8 %all-gather.7.cloned.1.call-done = bf16[128,128,64]{1,2,0:T(8,128)(2,1)} async-done(((bf16[32,128,64]{1,2,0:T(8,128)(2,1)}), bf16[128,128,64]{1,2,0:T(8,128)(2,1)}) %all-gather.7.cloned.1.call-update) | async-done | bytes 2097168 | tf_op jit(solution)/shard_map/all_gather | solution.py:18
  61.8 24.2 %while.14 = (s32[]{:T(128)}, f32[32,128,64]{2,1,0:T(8,128)}, s32[]{:T(128)}, bf16[4,32]{1,0:T(4,128)(2,1)S(1)}, bf16[4,32,128,64]{2,3,1,0:T(8,128)(2,1)}, /*index=5*/s32[]{:T(128)}, s32[]{:T(128)}) while((s32[]{:T(128)}, f32[32,128,64]{2,1,0:T(8,128)}, s32[]{:T(128)}, bf16[4,32]{1,0:T(4,128)(2,1)S(1)}, ...), condition=%wide.region_3.4_spmd.clone, body=%wide.region_2.3_spmd.clone.sunk | while | flops 1310756 | bytes 4719017 | solution.py:35
  62.9 1.4 copy.105
  64.3 2.9 fusion.81
  68.3 1.4 copy.105
  69.6 4.0 fusion.81
  74.8 1.4 copy.105
  76.2 3.8 fusion.81
  82.5 3.6 fusion.81
  86.1 3.6 fusion.60
  89.7 7.9 %fusion.18 = f32[256,32,64]{0,2,1:T(8,128)} fusion(bf16[256,32,64]{0,2,1:T(8,128)(2,1)S(1)} %bitcast.116, f32[32,64,256]{2,1,0:T(8,128)S(1)} %fusion.60, f32[256,256]{1,0:T(8,128)S(1)} %copy-done.4, f32[256,32]{0,1:T(8,128)S(1)} %bitcast_bitcast_fusion, pred[256,256]{1,0:T(8,128)(4,1)S(1)} %iota_compare_fusion, f32[32]{0:T(128)S(1)} %copy-done.10, ...), kind=kOutput, calls=%fused_computation.26 | convolution fusion | flops 1623719936 | bytes 5636224 | tf_op jit(solution)/shard_map/tsh,shp->thp/dot_general | solution.py:76
  97.6 2.9 copy.79
  100.5 3.7 fusion.67
  104.3 4.0 mul.106
  108.3 2.2 reduce_sum.27
  111.2 2.2 copy.91
  113.4 235.9 %all-gather.5.cloned.1.call-done = bf16[2048,4096]{1,0:T(8,128)(2,1)} async-done(((bf16[2048,1024]{1,0:T(8,128)(2,1)}), bf16[2048,4096]{1,0:T(8,128)(2,1)}) %all-gather.5.cloned.1.call-update) | async-done | bytes 16777232 | tf_op jit(solution)/shard_map/all_gather | solution.py:95
  349.3 13.4 %convolution_convert_fusion = bf16[256,4096]{1,0:T(8,128)(2,1)} fusion(bf16[2048,4096]{1,0:T(8,128)(2,1)} %all-gather.5.cloned.1.call-done, f32[256,2048]{1,0:T(8,128)} %bitcast.119, f32[2048]{0:T(1024)S(1)} %copy-done.8, f32[256,2048]{1,0:T(8,128)} %copy.79, bf16[256,2048]{1,0:T(8,128)(2,1)} %param.23), kind=kOutput, calls=%fused_computation.11 | convolution fusion | flops 4300734464 | bytes 24125440 | tf_op jit(solution)/shard_map/dot_general | solution.py:93
  364.6 27.3 %reduce-scatter.2.cloned.1.call-done = bf16[256,1024]{1,0:T(8,128)(2,1)} async-done(((bf16[256,4096]{1,0:T(8,128)(2,1)}), bf16[256,1024]{1,0:T(8,128)(2,1)}) %reduce-scatter.2.cloned.1.call-update) | async-done | bytes 524304 | tf_op jit(solution)/shard_map/reduce_scatter | solution.py:98
  392.0 3.3 convolution_convert_fusion.1
  396.6 5.9 %psum.22 = bf16[256]{0:T(256)(128)(2,1)S(1)} all-reduce(bf16[256]{0:T(256)(128)(2,1)S(1)} %multiply_reduce_fusion), channel_id=1, replica_groups=mesh['groups'=2,'ctx'=4,'heads'=4] {'heads'}, use_global_device_ids=true, to_apply=%region_12.13 | all-reduce | flops 256 | bytes 1024 | tf_op jit(solution)/shard_map/psum | solution.py:107
  402.5 25.3 %all-reduce.3.cloned.1.call-done = bf16[256,1024]{1,0:T(8,128)(2,1)} async-done(((bf16[256,1024]{1,0:T(8,128)(2,1)}), bf16[256,1024]{1,0:T(8,128)(2,1)}) %all-reduce.3.cloned.1.call-update) | async-done | bytes 524304 | tf_op jit(solution)/shard_map/psum | solution.py:106
  429.2 10.4 %all_to_all.10 = bf16[4,2,16,1024]{3,2,1,0:T(8,128)(2,1)S(1)} all-to-all(bf16[4,2,16,1024]{3,2,1,0:T(8,128)(2,1)S(1)} %bitcast.120), channel_id=1, replica_groups=mesh['groups'=2,'ctx'=4,'heads'=4] {'ctx'}, dimensions={0} | all-to-all | bytes 524288 | tf_op jit(solution)/shard_map/all_to_all | solution.py:128
  439.6 3.9 fusion.41
  444.3 31.8 %all-reduce.5.cloned.1.call-done = bf16[4,2,16,1024]{3,2,0,1:T(8,128)(2,1)} async-done(((bf16[4,2,16,1024]{3,2,0,1:T(8,128)(2,1)}), bf16[4,2,16,1024]{3,2,0,1:T(8,128)(2,1)}) %all-reduce.5.cloned.1.call-update) | async-done | bytes 262160 | tf_op jit(solution)/shard_map/psum | solution.py:129
  476.1 1.7 copy.83
  477.8 4.7 all-to-all-start.1
  483.8 4.3 all-to-all-done.1
  488.1 3.3 fusion.27
  (72 shorter events, 17.2 us)
Async XLA Ops:
  6.5 433.1 %copy-start = (bf16[2,672,1024]{2,1,0:T(8,128)(2,1)S(1)}, bf16[2,672,1024]{2,1,0:T(8,128)(2,1)}, u32[]{:S(2)}) copy-start(bf16[2,672,1024]{2,1,0:T(8,128)(2,1)} %param.30) | copy-start | bytes 8257540
  6.5 4.4 copy-start.5
  6.5 55.3 %all-gather.7.cloned.1.call-start = ((), (), s32[]{:S(2)}) async-start(), calls=%async_computation.7 | async-start | bytes 2621440 | tf_op jit(solution)/shard_map/all_gather | solution.py:18
  14.1 11.0 %copy-start.3 = (bf16[256,128]{1,0:T(8,128)(2,1)S(1)}, bf16[256,128]{1,0:T(8,128)(2,1)}, u32[]{:S(2)}) copy-start(bf16[256,128]{1,0:T(8,128)(2,1)} %param.21) | copy-start | bytes 196612
  14.1 335.2 %all-gather.5.cloned.1.call-start = ((), (), s32[]{:S(2)}) async-start(), calls=%async_computation.3 | async-start | bytes 20971520 | tf_op jit(solution)/shard_map/all_gather | solution.py:95
  14.9 377.1 %reduce-scatter.2.cloned.1.call-start = ((), (), s32[]{:S(2)}) async-start(), calls=%async_computation.4 | async-start | bytes 2621440 | tf_op jit(solution)/shard_map/reduce_scatter | solution.py:98
  86.1 3.6 copy-start.1
  86.1 3.6 copy-start.4
  86.1 3.6 copy-start.10
  111.2 238.2 %copy-start.8 = (f32[2048]{0:T(1024)S(1)}, f32[2048]{0:T(1024)}, u32[]{:S(2)}) copy-start(f32[2048]{0:T(1024)} %param.24) | copy-start | bytes 24580
  362.7 0.7 copy-start.6
  362.7 29.2 %copy-start.2 = (bf16[256,1024]{1,0:T(8,128)(2,1)S(1)}, bf16[256,1024]{1,0:T(8,128)(2,1)}, u32[]{:S(2)}) copy-start(bf16[256,1024]{1,0:T(8,128)(2,1)} %param.26) | copy-start | bytes 1572868
  362.7 29.2 %copy-start.9 = (f32[1024]{0:T(1024)S(1)}, f32[1024]{0:T(1024)}, u32[]{:S(2)}) copy-start(f32[1024]{0:T(1024)} %param.27) | copy-start | bytes 12292
  362.8 65.0 %all-reduce.3.cloned.1.call-start = ((), (), s32[]{:S(2)}) async-start(), calls=%async_computation.5 | async-start | bytes 1048576 | tf_op jit(solution)/shard_map/psum | solution.py:106
  363.5 31.7 %copy-start.7 = (pred[256,8]{0,1:T(8,128)(4,1)}, pred[256,8]{0,1:T(8,128)(4,1)S(1)}, u32[]{:S(2)}) copy-start(pred[256,8]{0,1:T(8,128)(4,1)S(1)} %get-tuple-element.165) | copy-start | bytes 6148
  395.3 80.8 %all-reduce.5.cloned.1.call-start = ((), (), s32[]{:S(2)}) async-start(), calls=%async_computation.6 | async-start | bytes 524288 | tf_op jit(solution)/shard_map/psum | solution.py:129
  477.8 10.4 %all-to-all-start.1 = ((bf16[4,2,16,1024]{3,2,1,0:T(8,128)(2,1)}), bf16[4,2,16,1024]{3,2,1,0:T(8,128)(2,1)S(1)}, u32[]{:S(2)}, u32[]{:S(2)}) async-start(bf16[4,2,16,1024]{3,2,1,0:T(8,128)(2,1)} %copy.83), calls=%async_computation.2 | async-start | bytes 524288 | tf_op jit(solution)/shard_map/all_to_all | solution.py:132
Sparse Core Ops, SparseCore 0:
  14.2 47.5 all-gather.6
  63.4 285.9 all-gather.4
  362.9 29.0 reduce-scatter.1
  395.4 32.3 all-reduce.2
  443.7 32.4 all-reduce.4
where the time goes:
time: 503 us; the launch traced here: 498 us
  waiting for transfers between devices  361 us (72%)
  matrix products  40.9 us (8%)
  blocking collectives  26.2 us (5%)
  local copies, waits for them, and re-layouts  25.8 us (5%)
  other arithmetic  25.5 us (5%)
  between operations  13.3 us (3%)
  starting transfers between devices  5.04 us (1%)
    all_gather x1, waiting for transfers between devices, local(): lax.all_gather(out_weight, 'ctx', axis=1, tiled=True)  236 us
    all_gather x1, waiting for transfers between devices, prefix(): lax.all_gather(part.astype(kind), axis)  35.8 us
    psum x1, waiting for transfers between devices, local(): lax.psum(expert_apply(incoming, expert_up, expert_down).astype(jnp.bfloat...  31.8 us
    reduce_scatter x1, waiting for transfers between devices, local(): lax.psum_scatter(partial_value.astype(jnp.bfloat16), 'heads', scatter_dim...  27.3 us
    psum x1, waiting for transfers between devices, local(): lax.psum(latent_part.astype(jnp.bfloat16), 'heads').astype(jnp.float32)  25.3 us
    select_n x4, other arithmetic, step(): return jax.tree.map(lambda a, b: jnp.where(reached, a, b), new, before)  14.3 us
    dot_general x1, matrix products, local(): jnp.dot(normed, lax.all_gather(out_weight, 'ctx', axis=1, tiled=True), pr...  13.4 us
    all_to_all x1, blocking collectives, local(): lax.all_to_all(outgoing, 'ctx', split_axis=0, concat_axis=0, tiled=True)  10.4 us
  transfers between devices with their start and end apart: 6, of which 6 were waited for; matrix products, arithmetic and copies ran while one was open for 11% of the time, Pallas kernels for 0%

commit v1 on v0

v1 whole, which is shorter than its diff:
```python
import functools

import jax
import jax.numpy as jnp
from jax import lax
from jax.experimental import pallas as pl
from jax.experimental.pallas import tpu as pltpu
from jax.sharding import PartitionSpec as P

D = 4096
GRP = 1024
LAT = 1024
CAP = 16


epsilon = 1e-05


MESH = pl.DeviceIdType.MESH
BF = jnp.bfloat16
F32 = jnp.float32


def vmem(count=1):
    return [pl.BlockSpec(memory_space=pltpu.VMEM)] * count


def greet(device):
    pl.semaphore_signal(
        pltpu.get_barrier_semaphore(), inc=1, device_id=device, device_id_type=MESH
    )


def greeted(count):
    pl.semaphore_wait(pltpu.get_barrier_semaphore(), count)


def one_if(condition):
    return jnp.where(condition, 1, 0)


def remote(src, dst, send, recv, device):
    return pltpu.make_async_remote_copy(
        src_ref=src, dst_ref=dst, send_sem=send, recv_sem=recv, device_id=device, device_id_type=MESH
    )


def pair_wide(first, second, width):
    lane = lax.broadcasted_iota(jnp.int32, (first.shape[0], 2 * width), 1)
    return jnp.where(lane < width, first, second)


def scan_kernel(width, x_ref, col_ref, row_ref, write_ref, read_ref, skip_ref, mixed_ref, state_ref, decay_ref, inter):
    rows = x_ref.shape[0]
    t = lax.broadcasted_iota(jnp.int32, (rows, rows), 0)
    s = lax.broadcasted_iota(jnp.int32, (rows, rows), 1)
    causal = t >= s

    @pl.when(pl.program_id(0) == 0)
    def _():
        product = lax.dot_general(
            read_ref[...], write_ref[...], (((1,), (1,)), ((), ())), preferred_element_type=F32
        )
        inter[...] = jnp.where(causal, product, 0.0)

    x = x_ref[...]
    outs, tails, ends = [], [], []
    for j in range(2):
        col = col_ref[0, :, j : j + 1]
        row = row_ref[0, j : j + 1, :]
        last = row_ref[0, j : j + 1, rows - 1 : rows]
        spread = jnp.where(causal, col - row, 0.0)
        mixing = (jnp.exp(-spread) * inter[...]).astype(BF)
        outs.append(
            jnp.dot(mixing, x[:, j * width : (j + 1) * width], preferred_element_type=F32)
        )
        tails.append(jnp.exp(col - last))
        ends.append(jnp.exp(-last))
    wide = x.astype(F32)
    mixed_ref[...] = jnp.concatenate(outs, axis=1) + skip_ref[...] * wide
    scaled = (wide * pair_wide(tails[0], tails[1], width)).astype(BF)
    state_ref[...] = lax.dot_general(
        write_ref[...], scaled, (((0,), (0,)), ((), ())), preferred_element_type=F32
    )
    decay_ref[...] = pair_wide(ends[0], ends[1], width)


def chain_kernel(n, chunks, state_ref, decay_ref, prior_ref, landed, outgoing, send_sem, recv_sem):
    me = lax.axis_index("ctx")
    size = state_ref.shape[1] // chunks
    has_prev, has_next = me > 0, me < n - 1
    prev, after = jnp.maximum(me - 1, 0), jnp.minimum(me + 1, n - 1)
    pl.when(has_prev)(lambda: greet({"ctx": prev}))
    pl.when(has_next)(lambda: greet({"ctx": after}))
    greeted(one_if(has_prev) + one_if(has_next))

    def copy(k):
        return remote(
            outgoing.at[k], landed.at[k], send_sem.at[k], recv_sem.at[k], {"ctx": after}
        )

    for k in range(chunks):
        part = pl.ds(k * size, size)

        @pl.when(me == 0)
        def _():
            prior_ref[:, part] = jnp.zeros((state_ref.shape[0], size), BF)

            if n > 1:
                outgoing[k] = state_ref[:, part].astype(BF)

        @pl.when(has_prev)
        def _():
            copy(k).wait_recv()
            came = landed[k]
            prior_ref[:, part] = came
            outgoing[k] = (came.astype(F32) * decay_ref[:, part] + state_ref[:, part]).astype(BF)

        pl.when(has_next)(lambda: copy(k).start())
    for k in range(chunks):
        pl.when(has_next)(lambda: copy(k).wait_send())


def gate_kernel(width, mixed_ref, prior_ref, col_ref, read_ref, gate_ref, gain_ref, normed_ref, gated):
    rows = mixed_ref.shape[0]
    pairs = col_ref.shape[0]
    squares = jnp.zeros((rows, 2 * width), F32)
    for p in range(pairs):
        part = slice(p * 2 * width, (p + 1) * 2 * width)
        reach = pair_wide(
            jnp.exp(-col_ref[p, :, 0:1]), jnp.exp(-col_ref[p, :, 1:2]), width
        )
        carried = jnp.dot(read_ref[...], prior_ref[:, part], preferred_element_type=F32) * reach
        gate = gate_ref[:, part].astype(F32)
        value = (mixed_ref[:, part] + carried) * (gate / (1.0 + jnp.exp(-gate)))
        gated[:, part] = value
        squares = squares + value * value
    scale = lax.rsqrt(jnp.sum(squares, axis=1, keepdims=True) / (pairs * 2 * width) + epsilon)
    normed_ref[...] = (gated[...] * scale * gain_ref[...]).astype(BF)


def project_kernel(
    n, heads, normed_ref, weight_ref, out_ref,
    blocks, parts, gathered, summed, final,
    up_send, up_recv, down_send, down_recv, part_send, part_recv, sum_send, sum_recv,
):
    me, head = lax.axis_index("ctx"), lax.axis_index("heads")
    share = n // heads
    column_head = me // share
    rows, width = normed_ref.shape[0], weight_ref.shape[1]
    has_prev, has_next = me > 0, me < n - 1
    prev, after = jnp.maximum(me - 1, 0), jnp.minimum(me + 1, n - 1)

    def holder(j):
        return head * share + j, column_head

    def other(j):
        ctx, side = holder(j)
        return jnp.logical_or(ctx != me, side != head)

    pl.when(has_prev)(lambda: greet({"ctx": prev}))
    pl.when(has_next)(lambda: greet({"ctx": after}))
    for k in range(1, heads):
        greet({"heads": (head + k) % heads})
    count = one_if(has_prev) + one_if(has_next) + heads - 1
    for j in range(share):
        ctx, side = holder(j)
        pl.when(other(j))(lambda: greet({"ctx": ctx, "heads": side}))
        count = count + one_if(other(j))
    greeted(count)

    def upward(s, src):
        return remote(src, blocks.at[me - s], up_send.at[s], up_recv.at[s], {"ctx": after})

    def downward(s, src):
        return remote(src, blocks.at[me + s], down_send.at[s], down_recv.at[s], {"ctx": prev})

    def part_copy(b, target):
        return remote(
            parts.at[b], gathered.at[b % share, head], part_send.at[b],
            part_recv.at[b % share, head], {"heads": target},
        )

    def multiply(b, src):
        step = min(width, 256)
        for lo in range(0, width, step):
            parts[b, :, lo : lo + step] = jnp.dot(
                src[...], weight_ref[:, lo : lo + step], preferred_element_type=F32
            ).astype(BF)
        target = b // share
        pl.when(target != head)(lambda: part_copy(b, target).start())

    pl.when(has_next)(lambda: upward(0, normed_ref).start())
    pl.when(has_prev)(lambda: downward(0, normed_ref).start())
    multiply(me, normed_ref)

    for s in range(1, n):
        low, high = me - s, me + s
        low_ok, high_ok = low >= 0, high < n

        @pl.when(low_ok)
        def _():
            remote(
                normed_ref, blocks.at[low], up_send.at[s - 1], up_recv.at[s - 1], {"ctx": after}
            ).wait_recv()
            pl.when(has_next)(lambda: upward(s, blocks.at[low]).start())
            multiply(low, blocks.at[low])

        @pl.when(high_ok)
        def _():
            remote(
                normed_ref, blocks.at[high], down_send.at[s - 1], down_recv.at[s - 1], {"ctx": prev}
            ).wait_recv()
            pl.when(has_prev)(lambda: downward(s, blocks.at[high]).start())
            multiply(high, blocks.at[high])

    def sum_copy(j):
        ctx, side = holder(j)
        return remote(
            summed.at[j], final.at[me % share], sum_send.at[j], sum_recv.at[me % share],
            {"ctx": ctx, "heads": side},
        )

    for j in range(share):
        mine = head * share + j
        total = parts[mine].astype(F32)
        for k in range(1, heads):
            source = (head + k) % heads
            remote(
                parts.at[mine], gathered.at[j, source], part_send.at[mine],
                part_recv.at[j, source], {"heads": source},
            ).wait_recv()
            total = total + gathered[j, source].astype(F32)
        summed[j] = total.astype(BF)
        pl.when(other(j))(lambda: sum_copy(j).start())

    for i in range(share):
        ctx, side = holder(i)
        here = slice(i * width, (i + 1) * width)

        @pl.when(other(i))
        def _():
            remote(
                summed.at[i], final.at[i], sum_send.at[i], sum_recv.at[i],
                {"ctx": ctx, "heads": side},
            ).wait_recv()
            out_ref[:, here] = final[i].astype(F32)

        @pl.when(jnp.logical_not(other(i)))
        def _():
            out_ref[:, here] = summed[me % share].astype(F32)

    for s in range(n):
        pl.when(jnp.logical_and(has_next, me - s >= 0))(
            lambda: upward(s, normed_ref).wait_send()
        )
        pl.when(jnp.logical_and(has_prev, me + s < n))(
            lambda: downward(s, normed_ref).wait_send()
        )
    for b in range(n):
        pl.when(b // share != head)(lambda: part_copy(b, b // share).wait_send())
    for j in range(share):
        pl.when(other(j))(lambda: sum_copy(j).wait_send())


def slots_kernel(
    n, heads, width, features, src_ref, out_ref,
    first, middle, second, third,
    first_send, first_recv, second_send, second_recv, third_send, third_recv,
):
    me, head = lax.axis_index("ctx"), lax.axis_index("heads")

    for k in range(1, heads):
        greet({"heads": (head + k) % heads})
    for k in range(1, n):
        greet({"ctx": (me + k) % n})
    greeted(heads + n - 2)

    def first_copy(k):
        to = (head + k) % heads
        return remote(
            src_ref.at[to], first.at[k], first_send.at[k], first_recv.at[k], {"heads": to}
        )

    def second_copy(k):
        to = (me + k) % n
        return remote(
            middle.at[to], second.at[me], second_send.at[k], second_recv.at[k], {"ctx": to}
        )

    def third_copy(k):
        to = (head + k) % heads
        return remote(second, third.at[k], third_send.at[k], third_recv.at[k], {"heads": to})

    for k in range(1, heads):
        first_copy(k).start()
    total = src_ref[head].astype(F32)
    for k in range(1, heads):
        first_copy(k).wait_recv()
        total = total + first[k].astype(F32)
    if src_ref.shape[-1] > width:
        power = total[:, :, width : width + 1]
        total = total[:, :, :width] * lax.rsqrt(power / features + epsilon)
    middle[...] = total.astype(BF)
    for k in range(1, n):
        second_copy(k).start()
    second[me] = middle[me]
    for k in range(1, n):
        second_copy(k).wait_recv()
    for k in range(1, heads):
        third_copy(k).start()
    out_ref[head] = second[...]
    for k in range(1, heads):
        third_copy(k).wait_recv()
        out_ref[(head + heads - k) % heads] = third[k]
    for k in range(1, heads):
        first_copy(k).wait_send()
        third_copy(k).wait_send()
    for k in range(1, n):
        second_copy(k).wait_send()


def reaching(collective_id):
    return pltpu.CompilerParams(
        collective_id=collective_id, has_side_effects=True, vmem_limit_bytes=48 * 1024 * 1024
    )


def dma(*shape):
    return pltpu.SemaphoreType.DMA(shape)


def through_slots(pieces, width, features, collective_id):
    heads, n, rows, wide = pieces.shape
    return pl.pallas_call(
        functools.partial(slots_kernel, n, heads, width, features),
        out_shape=jax.ShapeDtypeStruct((heads, n, rows, width), BF),
        in_specs=vmem(),
        out_specs=vmem()[0],
        scratch_shapes=[
            pltpu.VMEM((heads, n, rows, wide), BF),
            pltpu.VMEM((n, rows, width), BF),
            pltpu.VMEM((n, rows, width), BF),
            pltpu.VMEM((heads, n, rows, width), BF),
            dma(heads), dma(heads), dma(n), dma(n), dma(heads), dma(heads),
        ],
        compiler_params=reaching(collective_id),
    )(pieces)


def mixer(ssm_input, decay_log, state_write, state_read, skip_scale, gate_input, ssm_gain):
    n = lax.axis_size("ctx")
    rows, columns = ssm_input.shape
    head_count = decay_log.shape[1]
    width = columns // head_count
    pairs, states = head_count // 2, state_write.shape[1]
    cumulative = jnp.cumsum(decay_log, axis=0)
    by_row = cumulative.T.reshape(pairs, 2, rows)
    by_col = by_row.transpose(0, 2, 1)
    skip = jnp.repeat(skip_scale, width).reshape(1, columns)
    span = 2 * width
    whole = lambda p: (0, 0)
    mixed, state, decay = pl.pallas_call(
        functools.partial(scan_kernel, width),
        grid=(pairs,),
        out_shape=(
            jax.ShapeDtypeStruct((rows, columns), F32),
            jax.ShapeDtypeStruct((states, columns), F32),
            jax.ShapeDtypeStruct((1, columns), F32),
        ),
        in_specs=[
            pl.BlockSpec((rows, span), lambda p: (0, p)),
            pl.BlockSpec((1, rows, 2), lambda p: (p, 0, 0)),
            pl.BlockSpec((1, 2, rows), lambda p: (p, 0, 0)),
            pl.BlockSpec((rows, states), whole),
            pl.BlockSpec((rows, states), whole),
            pl.BlockSpec((1, span), lambda p: (0, p)),
        ],
        out_specs=(
            pl.BlockSpec((rows, span), lambda p: (0, p)),
            pl.BlockSpec((states, span), lambda p: (0, p)),
            pl.BlockSpec((1, span), lambda p: (0, p)),
        ),
        scratch_shapes=[pltpu.VMEM((rows, rows), F32)],
    )(ssm_input, by_col, by_row, state_write, state_read, skip)
    chunks = 4
    prior = pl.pallas_call(
        functools.partial(chain_kernel, n, chunks),
        out_shape=jax.ShapeDtypeStruct((states, columns), BF),
        in_specs=vmem(2),
        out_specs=vmem()[0],
        scratch_shapes=[
            pltpu.VMEM((chunks, states, columns // chunks), BF),
            pltpu.VMEM((chunks, states, columns // chunks), BF),
            dma(chunks),
            dma(chunks),
        ],
        compiler_params=reaching(1),
    )(state, decay)
    group_pairs = GRP // span
    at = lambda g: (0, g)
    return pl.pallas_call(
        functools.partial(gate_kernel, width),
        grid=(columns // GRP,),
        out_shape=jax.ShapeDtypeStruct((rows, columns), BF),
        in_specs=[
            pl.BlockSpec((rows, GRP), at),
            pl.BlockSpec((states, GRP), at),
            pl.BlockSpec((group_pairs, rows, 2), lambda g: (g, 0, 0)),
            pl.BlockSpec((rows, states), whole),
            pl.BlockSpec((rows, GRP), at),
            pl.BlockSpec((1, GRP), at),
        ],
        out_specs=pl.BlockSpec((rows, GRP), at),
        scratch_shapes=[pltpu.VMEM((rows, GRP), F32)],
    )(mixed, prior, by_col, state_read, gate_input, ssm_gain.reshape(1, columns))


def project(normed, weight):
    n, heads = lax.axis_size("ctx"), lax.axis_size("heads")
    rows, width = normed.shape[0], weight.shape[1]
    share = n // heads
    block = (rows, width)
    return pl.pallas_call(
        functools.partial(project_kernel, n, heads),
        out_shape=jax.ShapeDtypeStruct((rows, share * width), F32),
        in_specs=vmem(2),
        out_specs=vmem()[0],
        scratch_shapes=[
            pltpu.VMEM((n,) + normed.shape, BF),
            pltpu.VMEM((n,) + block, BF),
            pltpu.VMEM((share, heads) + block, BF),
            pltpu.VMEM((share,) + block, BF),
            pltpu.VMEM((share,) + block, BF),
            dma(n), dma(n), dma(n), dma(n), dma(n), dma(share, heads), dma(share), dma(share),
        ],
        compiler_params=reaching(2),
    )(normed, weight)


def local(
    ssm_input,
    decay_log,
    state_write,
    state_read,
    skip_scale,
    gate_input,
    ssm_gain,
    out_weight,
    residual_in,
    moe_gain,
    down_latent,
    expert_up,
    expert_down,
    up_latent,
    expert_ids,
    combine_fixed,
):
    row_count = ssm_input.shape[0]
    n, heads = lax.axis_size("ctx"), lax.axis_size("heads")
    features = residual_in.shape[1] * heads
    latent_width = down_latent.shape[1]
    piece = latent_width // heads
    experts_here = expert_up.shape[0]
    wave_size = experts_here * n
    slot_rows = experts_here * CAP

    matches = expert_ids[:, :, None] == jnp.arange(wave_size)[None, None, :]
    chosen = jnp.any(matches, axis=1).astype(jnp.int32)
    weight_fixed = jnp.sum(jnp.where(matches, combine_fixed[:, :, None], 0), axis=1)
    slot_index = jnp.cumsum(chosen, axis=0) - 1
    placed = (chosen[:, :, None] == 1) & (slot_index[:, :, None] == jnp.arange(CAP)[None, None, :])
    route_weight = (weight_fixed.astype(F32) / 65536.0).astype(BF)
    combine_table = jnp.where(placed, route_weight[:, :, None], jnp.zeros((), BF)).reshape(
        row_count, wave_size * CAP
    )
    placed = placed.astype(BF).reshape(row_count, wave_size * CAP)

    normed = mixer(
        ssm_input, decay_log, state_write, state_read, skip_scale, gate_input, ssm_gain
    )
    residual = residual_in.astype(F32) + project(normed, out_weight)
    scaled = (residual * moe_gain).astype(BF)
    latent_part = jnp.dot(scaled, down_latent, preferred_element_type=F32).astype(BF)
    squares = jnp.sum(residual * residual, axis=1).astype(BF)
    side = jnp.concatenate(
        [latent_part, jnp.broadcast_to(squares[:, None], (row_count, 128))], axis=1
    )
    slots = lax.dot_general(
        placed, side, (((0,), (0,)), ((), ())), preferred_element_type=F32
    ).astype(BF)
    slots = slots.reshape(n, slot_rows, latent_width + 128)
    pieces = jnp.stack(
        [
            jnp.concatenate(
                [slots[:, :, h * piece : (h + 1) * piece], slots[:, :, latent_width:]], axis=2
            )
            for h in range(heads)
        ]
    )
    incoming = through_slots(pieces, piece, features, 3)
    incoming = incoming.reshape(heads, n, experts_here, CAP, piece).transpose(2, 1, 3, 0, 4)
    incoming = incoming.reshape(experts_here, n * CAP, latent_width)
    hidden = jnp.einsum("esl,elf->esf", incoming, expert_up, preferred_element_type=F32)
    hidden = (jnp.maximum(hidden, 0.0) ** 2).astype(BF)
    expert_out = jnp.einsum("esf,efl->esl", hidden, expert_down, preferred_element_type=F32)
    expert_out = expert_out.astype(BF).reshape(experts_here, n, CAP, heads, piece)
    expert_out = expert_out.transpose(3, 1, 0, 2, 4).reshape(heads, n, slot_rows, piece)
    returned = through_slots(expert_out, piece, features, 4)
    returned = returned.transpose(1, 2, 0, 3).reshape(wave_size * CAP, latent_width)
    combined = jnp.dot(combine_table, returned, preferred_element_type=F32)
    moe_out = jnp.dot(combined.astype(BF), up_latent, preferred_element_type=F32)
    return (residual + moe_out).astype(BF)


def solution(mesh):
    placed = (
        P(("groups", "ctx"), "heads"),
        P(("groups", "ctx"), "heads"),
        P(("groups", "ctx"), None),
        P(("groups", "ctx"), None),
        P("heads"),
        P(("groups", "ctx"), "heads"),
        P("heads"),
        P("heads", "ctx"),
        P(("groups", "ctx"), "heads"),
        P("heads"),
        P("heads", None),
        P("ctx", None, "heads"),
        P("ctx", "heads", None),
        P(None, "heads"),
        P(("groups", "ctx"), None),
        P(("groups", "ctx"), None),
    )
    return jax.shard_map(
        local, mesh=mesh, in_specs=placed, out_specs=P(("groups", "ctx"), "heads"), check_vma=False
    )
```

time: 503 us -> 202 us (0.40)
  waiting for transfers between devices: 361 us -> 0 us
  Pallas kernels: 0 us -> 177 us
  matrix products: 40.9 us -> 10.2 us
  blocking collectives: 26.2 us -> 0 us
  other arithmetic: 25.5 us -> 2.54 us
  local copies, waits for them, and re-layouts: 25.8 us -> 11.8 us
  between operations: 13.3 us -> 0.28 us
  starting transfers between devices: 5.04 us -> 0 us
    all_gather x2 -> x0, waiting for transfers between devices: 272 us -> none  [the longest x1 236 us: local(): lax.all_gather(out_weight, 'ctx', axis=1, tiled=True)]
    pallas_call x0 -> x6, Pallas kernels: none -> 177 us  [the longest x1 99.8 us: project(): pl.pallas_call(functools.partial(project_kernel, n, heads), out_shape=jax...]
    psum x2 -> x0, waiting for transfers between devices: 57.1 us -> none  [the longest x1 31.8 us: local(): lax.psum(expert_apply(incoming, expert_up, expert_down).astype(jnp.bfloat...]
    dot_general x9 -> x4, matrix products: 40.9 us -> 10.2 us  [the longest x1 3.9 us: local(): jnp.einsum('esf,efl->esl', hidden, expert_down, preferred_element_type=F32)]
    reduce_scatter x1 -> x0, waiting for transfers between devices: 27.3 us -> none  [local(): lax.psum_scatter(partial_value.astype(jnp.bfloat16), 'heads', scatter_dim...]
    select_n x5 -> x1, other arithmetic: 15.6 us -> 0.65 us  [local(): jnp.where(placed, route_weight[:, :, None], jnp.zeros((), BF))]
    all_to_all x1 -> x0, blocking collectives: 10.4 us -> none  [local(): lax.all_to_all(outgoing, 'ctx', split_axis=0, concat_axis=0, tiled=True)]
    all_gather x1 -> x0, blocking collectives: 9.96 us -> none  [prefix(): lax.all_gather(part.astype(kind), axis)]
  transfers between devices with their start and end apart: 6 -> 0, of which waited for: 6 -> 0; matrix products, arithmetic and copies ran while one was open for 11% -> 0% of each run, Pallas kernels for 0% -> 0%
where the time goes in v1:
time: 202 us
  Pallas kernels  177 us (88%)
  local copies, waits for them, and re-layouts  11.8 us (6%)
  matrix products  10.2 us (5%)
  other arithmetic  2.54 us (1%)
    pallas_call x1, Pallas kernels, project(): pl.pallas_call(functools.partial(project_kernel, n, heads), out_shape=jax...  99.8 us
    pallas_call x2, Pallas kernels, through_slots(): pl.pallas_call(functools.partial(slots_kernel, n, heads, width, features)...  45.8 us
    pallas_call x1, Pallas kernels, mixer(): pl.pallas_call(functools.partial(scan_kernel, width), grid=(pairs,), out_...  13.5 us
    pallas_call x1, Pallas kernels, mixer(): pl.pallas_call(functools.partial(chain_kernel, n, chunks), out_shape=jax....  12.8 us
    pallas_call x1, Pallas kernels, mixer(): pl.pallas_call(functools.partial(gate_kernel, width), grid=(columns // GR...  4.85 us

profile of v1, /device:TPU:1, one launch (start us, length us, event | category | flops | bytes accessed | tf_op | source)
XLA Modules:
  0.0 201.6 jit_solution(975784123674868880)
XLA Ops:
  0.0 0.9 copy_bitcast_fusion.1
  0.9 0.6 reduce-window.14
  1.5 0.2 slice_reduce_fusion
  1.7 0.1 broadcast_add_fusion
  1.9 2.0 copy.32
  4.0 0.7 reshape_reshape.3.skip_ref
  4.6 13.5 %shard_map.154 = (f32[256,2048]{1,0:T(8,128)}, f32[128,2048]{1,0:T(8,128)}, f32[1,2048]{1,0:T(1,128)}) custom-call(bf16[256,2048]{1,0:T(8,128)(2,1)} %x_ref.1, f32[16,256,2]{2,1,0:T(8,128)} %bitcast.54, f32[16,2,256]{2,1,0:T(2,128)} %copy-done.8, bf16[256,128]{1,0:T(8,128)(2,1)} %write_ref.1, bf16[256,128]{1,0:T(8,128)(2,1)} %read_ref.3, ...), custom_call_target="tpu_custom_call" | custom-call | tf_op jit(solution)/shard_map/pallas_call | solution.py:363
  18.2 1.2 copy-done.4
  19.4 0.7 copy-done.5
  20.1 12.8 %shard_map.155.prior_ref = bf16[128,2048]{1,0:T(8,128)(2,1)S(1)} custom-call(f32[128,2048]{1,0:T(8,128)S(1)} %copy-done.4, f32[1,2048]{1,0:T(1,128)S(1)} %copy-done.5), custom_call_target="tpu_custom_call" | custom-call | tf_op jit(solution)/shard_map/pallas_call | solution.py:387
  32.9 0.8 copy-done.3
  33.7 4.8 %shard_map.156.normed_ref = bf16[256,2048]{1,0:T(8,128)(2,1)} custom-call(f32[256,2048]{1,0:T(8,128)} %get-tuple-element.8.mixed_ref, bf16[128,2048]{1,0:T(8,128)(2,1)} %copy-done.3, f32[16,256,2]{2,1,0:T(8,128)} %bitcast.55, bf16[256,128]{1,0:T(8,128)(2,1)} %read_ref.3, bf16[256,2048]{1,0:T(8,128)(2,1)} %gate_ref.1, f32[1,2048]{1,0:T(1,128)} %bitcast.63), custom_call_target="tpu_custom_call" | custom-call | tf_op jit(solution)/shard_map/pallas_call | solution.py:402
  38.6 1.2 copy-done.2
  39.8 99.8 %shard_map.157 = f32[256,1024]{1,0:T(8,128)S(1)} custom-call(bf16[256,2048]{1,0:T(8,128)(2,1)S(1)} %copy-done.2, bf16[2048,1024]{1,0:T(8,128)(2,1)} %weight_ref.1), custom_call_target="tpu_custom_call" | custom-call | tf_op jit(solution)/shard_map/pallas_call | solution.py:424
  139.6 1.5 convolution_convert_fusion.1
  141.1 0.2 multiply_reduce_fusion
  141.3 0.1 broadcast_in_dim.46
  141.5 0.6 reduce-window.16
  142.1 0.2 slice_reduce_fusion.1
  142.4 0.1 add_bitcast_fusion
  142.4 0.1 eq.66
  142.5 0.1 fusion.11
  142.6 1.3 convolution_convert_fusion
  144.1 29.8 %shard_map.158 = bf16[4,4,32,256]{3,2,1,0:T(8,128)(2,1)S(1)} custom-call(bf16[4,4,32,384]{3,2,1,0:T(8,128)(2,1)S(1)} %pad_maximum_fusion.src_ref), custom_call_target="tpu_custom_call" | custom-call | tf_op jit(solution)/shard_map/pallas_call | solution.py:335
  174.0 0.9 copy.40
  174.9 1.1 reshape.116
  176.0 3.9 %convolution_convert_fusion.3 = bf16[2,64,1024]{2,1,0:T(8,128)(2,1)} fusion(bf16[2,672,1024]{2,1,0:T(8,128)(2,1)S(1)} %copy-done, bf16[2,64,1024]{2,1,0:T(8,128)(2,1)S(1)} %reshape.116, bf16[2,1024,672]{1,2,0:T(8,128)(2,1)} %param.27), kind=kOutput, calls=%fused_computation.5 | convolution fusion | flops 352710656 | bytes 6029312 | tf_op jit(solution)/shard_map/esf,efl->esl/dot_general | solution.py:506
  179.9 1.1 reshape.117
  181.1 16.0 %shard_map.159 = bf16[4,4,32,256]{3,2,1,0:T(8,128)(2,1)S(1)} custom-call(bf16[4,4,32,256]{3,2,1,0:T(8,128)(2,1)S(1)} %bitcast.52), custom_call_target="tpu_custom_call" | custom-call | tf_op jit(solution)/shard_map/pallas_call | solution.py:335
  197.1 0.2 copy.35
  197.4 0.7 fusion.10
  198.0 3.5 %fusion = bf16[256,1024]{1,0:T(8,128)(2,1)} fusion(bf16[1024,1024]{1,0:T(8,128)(2,1)} %param.29, bf16[256,128]{0,1:T(8,128)(2,1)} %bitcast.62, bf16[128,1024]{1,0:T(8,128)(2,1)S(1)} %bitcast.56, f32[256,1024]{1,0:T(8,128)} %copy-done.1, bf16[256,1024]{1,0:T(8,128)(2,1)S(1)} %copy-done.6), kind=kOutput, calls=%fused_computation.3 | convolution fusion | flops 605290496 | bytes 4521984 | tf_op jit(solution)/shard_map/dot_general | solution.py:512
  (42 shorter events, 0.6 us)
Async XLA Ops:
  0.0 176.0 %copy-start = (bf16[2,672,1024]{2,1,0:T(8,128)(2,1)S(1)}, bf16[2,672,1024]{2,1,0:T(8,128)(2,1)}, u32[]{:S(2)}) copy-start(bf16[2,672,1024]{2,1,0:T(8,128)(2,1)} %param.28) | copy-start | bytes 8257540
  0.0 3.9 %copy-start.13 = (f32[32]{0:T(128)S(1)}, f32[32]{0:T(128)}, u32[]{:S(2)}) copy-start(f32[32]{0:T(128)} %param.20) | copy-start | bytes 388
  1.9 2.8 %copy-start.8 = (f32[16,2,256]{2,1,0:T(2,128)}, f32[16,2,256]{2,1,0:T(2,128)S(1)}, u32[]{:S(2)}) copy-start(f32[16,2,256]{2,1,0:T(2,128)S(1)} %reduce_window_sum.30.row_ref) | copy-start | bytes 98308
  18.2 1.2 copy-start.4
  19.4 0.7 copy-start.5
  32.9 0.8 copy-start.3
  38.6 1.2 copy-start.2
  39.8 99.8 %copy-start.6 = (bf16[256,1024]{1,0:T(8,128)(2,1)S(1)}, bf16[256,1024]{1,0:T(8,128)(2,1)}, u32[]{:S(2)}) copy-start(bf16[256,1024]{1,0:T(8,128)(2,1)} %param.24) | copy-start | bytes 1572868
  39.8 99.8 %copy-start.7 = (bf16[1024,1024]{1,0:T(8,128)(2,1)S(1)}, bf16[1024,1024]{1,0:T(8,128)(2,1)}, u32[]{:S(2)}) copy-start(bf16[1024,1024]{1,0:T(8,128)(2,1)} %param.26) | copy-start | bytes 6291460
  39.8 99.8 %copy-start.12 = (f32[1024]{0:T(1024)S(1)}, f32[1024]{0:T(1024)}, u32[]{:S(2)}) copy-start(f32[1024]{0:T(1024)} %param.25) | copy-start | bytes 12292
  139.6 1.5 copy-start.1
  139.6 1.9 copy-start.9
  181.0 16.3 %copy-start.10 = (s32[256,22]{0,1:T(8,128)S(1)}, s32[256,22]{0,1:T(8,128)}, u32[]{:S(2)}) copy-start(s32[256,22]{0,1:T(8,128)} %param.30) | copy-start | bytes 67588
  181.0 16.3 %copy-start.11 = (s32[256,22]{0,1:T(8,128)S(1)}, s32[256,22]{0,1:T(8,128)}, u32[]{:S(2)}) copy-start(s32[256,22]{0,1:T(8,128)} %param.31) | copy-start | bytes 67588

commit v2 on v1

--- a/solution.py
+++ b/solution.py
@@ -52,6 +52,7 @@
 
 def scan_kernel(width, x_ref, col_ref, row_ref, write_ref, read_ref, skip_ref, mixed_ref, state_ref, decay_ref, inter):
     rows = x_ref.shape[0]
+    band = rows // 2
     t = lax.broadcasted_iota(jnp.int32, (rows, rows), 0)
     s = lax.broadcasted_iota(jnp.int32, (rows, rows), 1)
     causal = t >= s
@@ -69,11 +70,16 @@
         col = col_ref[0, :, j : j + 1]
         row = row_ref[0, j : j + 1, :]
         last = row_ref[0, j : j + 1, rows - 1 : rows]
-        spread = jnp.where(causal, col - row, 0.0)
-        mixing = (jnp.exp(-spread) * inter[...]).astype(BF)
-        outs.append(
-            jnp.dot(mixing, x[:, j * width : (j + 1) * width], preferred_element_type=F32)
-        )
+        lane = x[:, j * width : (j + 1) * width]
+        bands = []
+        for lo in range(0, rows, band):
+            hi = lo + band
+            spread = jnp.where(causal[lo:hi, lo:hi], col[lo:hi] - row[:, lo:hi], 0.0)
+            if lo:
+                spread = jnp.concatenate([col[lo:hi] - row[:, :lo], spread], axis=1)
+            mixing = (jnp.exp(-spread) * inter[lo:hi, :hi]).astype(BF)
+            bands.append(jnp.dot(mixing, lane[:hi], preferred_element_type=F32))
+        outs.append(jnp.concatenate(bands, axis=0))
         tails.append(jnp.exp(col - last))
         ends.append(jnp.exp(-last))
     wide = x.astype(F32)
@@ -148,8 +154,8 @@
     share = n // heads
     column_head = me // share
     rows, width = normed_ref.shape[0], weight_ref.shape[1]
-    has_prev, has_next = me > 0, me < n - 1
-    prev, after = jnp.maximum(me - 1, 0), jnp.minimum(me + 1, n - 1)
+    prev, after = (me + n - 1) % n, (me + 1) % n
+    half = rows // 2
 
     def holder(j):
         return head * share + j, column_head
@@ -158,22 +164,34 @@
         ctx, side = holder(j)
         return jnp.logical_or(ctx != me, side != head)
 
-    pl.when(has_prev)(lambda: greet({"ctx": prev}))
-    pl.when(has_next)(lambda: greet({"ctx": after}))
+    greet({"ctx": prev})
+    greet({"ctx": after})
     for k in range(1, heads):
         greet({"heads": (head + k) % heads})
-    count = one_if(has_prev) + one_if(has_next) + heads - 1
+    count = heads + 1
     for j in range(share):
         ctx, side = holder(j)
         pl.when(other(j))(lambda: greet({"ctx": ctx, "heads": side}))
         count = count + one_if(other(j))
     greeted(count)
 
-    def upward(s, src):
-        return remote(src, blocks.at[me - s], up_send.at[s], up_recv.at[s], {"ctx": after})
-
-    def downward(s, src):
-        return remote(src, blocks.at[me + s], down_send.at[s], down_recv.at[s], {"ctx": prev})
+    def up_rows(s):
+        return pl.ds(0, half if 2 * s == n else rows)
+
+    def down_rows(s):
+        return pl.ds(half, half) if 2 * s == n else pl.ds(0, rows)
+
+    def upward(s, src, block):
+        part = up_rows(s)
+        return remote(
+            src.at[part], blocks.at[block, part], up_send.at[s], up_recv.at[s], {"ctx": after}
+        )
+
+    def downward(s, src, block):
+        part = down_rows(s)
+        return remote(
+            src.at[part], blocks.at[block, part], down_send.at[s], down_recv.at[s], {"ctx": prev}
+        )
 
     def part_copy(b, target):
         return remote(
@@ -181,38 +199,37 @@
             part_recv.at[b % share, head], {"heads": target},
         )
 
-    def multiply(b, src):
+    def multiply(b, src, start, size):
         step = min(width, 256)
         for lo in range(0, width, step):
-            parts[b, :, lo : lo + step] = jnp.dot(
-                src[...], weight_ref[:, lo : lo + step], preferred_element_type=F32
+            parts[b, start : start + size, lo : lo + step] = jnp.dot(
+                src[start : start + size, :], weight_ref[:, lo : lo + step],
+                preferred_element_type=F32,
             ).astype(BF)
+
+    def deliver(b):
         target = b // share
         pl.when(target != head)(lambda: part_copy(b, target).start())
 
-    pl.when(has_next)(lambda: upward(0, normed_ref).start())
-    pl.when(has_prev)(lambda: downward(0, normed_ref).start())
-    multiply(me, normed_ref)
-
-    for s in range(1, n):
-        low, high = me - s, me + s
-        low_ok, high_ok = low >= 0, high < n
-
-        @pl.when(low_ok)
-        def _():
-            remote(
-                normed_ref, blocks.at[low], up_send.at[s - 1], up_recv.at[s - 1], {"ctx": after}
-            ).wait_recv()
-            pl.when(has_next)(lambda: upward(s, blocks.at[low]).start())
-            multiply(low, blocks.at[low])
-
-        @pl.when(high_ok)
-        def _():
-            remote(
-                normed_ref, blocks.at[high], down_send.at[s - 1], down_recv.at[s - 1], {"ctx": prev}
-            ).wait_recv()
-            pl.when(has_prev)(lambda: downward(s, blocks.at[high]).start())
-            multiply(high, blocks.at[high])
+    reach = n // 2
+    upward(1, normed_ref, me).start()
+    downward(1, normed_ref, me).start()
+    multiply(me, normed_ref, 0, rows)
+    deliver(me)
+    for s in range(1, reach + 1):
+        low, high = (me + n - s) % n, (me + s) % n
+        upward(s, normed_ref, low).wait_recv()
+        if s < reach:
+            upward(s + 1, blocks.at[low], low).start()
+        downward(s, normed_ref, high).wait_recv()
+        if s < reach:
+            downward(s + 1, blocks.at[high], high).start()
+            multiply(low, blocks.at[low], 0, rows)
+            deliver(low)
+            multiply(high, blocks.at[high], 0, rows)
+        else:
+            multiply(high, blocks.at[high], 0, rows)
+        deliver(high)
 
     def sum_copy(j):
         ctx, side = holder(j)
@@ -250,13 +267,9 @@
         def _():
             out_ref[:, here] = summed[me % share].astype(F32)
 
-    for s in range(n):
-        pl.when(jnp.logical_and(has_next, me - s >= 0))(
-            lambda: upward(s, normed_ref).wait_send()
-        )
-        pl.when(jnp.logical_and(has_prev, me + s < n))(
-            lambda: downward(s, normed_ref).wait_send()
-        )
+    for s in range(1, reach + 1):
+        upward(s, normed_ref, me).wait_send()
+        downward(s, normed_ref, me).wait_send()
     for b in range(n):
         pl.when(b // share != head)(lambda: part_copy(b, b // share).wait_send())
     for j in range(share):
@@ -383,7 +396,7 @@
         ),
         scratch_shapes=[pltpu.VMEM((rows, rows), F32)],
     )(ssm_input, by_col, by_row, state_write, state_read, skip)
-    chunks = 4
+    chunks = 8
     prior = pl.pallas_call(
         functools.partial(chain_kernel, n, chunks),
         out_shape=jax.ShapeDtypeStruct((states, columns), BF),

time: 202 us -> 202 us (level)
  no operation moved by 1% of the time
where the time goes in v2:
time: 202 us; the launch traced here: 201 us
  Pallas kernels  176 us (87%)
  local copies, waits for them, and re-layouts  11.8 us (6%)
  matrix products  10.2 us (5%)
  other arithmetic  2.54 us (1%)
    pallas_call x1, Pallas kernels, project(): pl.pallas_call(functools.partial(project_kernel, n, heads), out_shape=jax...  98.5 us
    pallas_call x2, Pallas kernels, through_slots(): pl.pallas_call(functools.partial(slots_kernel, n, heads, width, features)...  46.7 us
    pallas_call x1, Pallas kernels, mixer(): pl.pallas_call(functools.partial(scan_kernel, width), grid=(pairs,), out_...  13.2 us
    pallas_call x1, Pallas kernels, mixer(): pl.pallas_call(functools.partial(chain_kernel, n, chunks), out_shape=jax....  12.9 us
    pallas_call x1, Pallas kernels, mixer(): pl.pallas_call(functools.partial(gate_kernel, width), grid=(columns // GR...  4.85 us

profile of v2, /device:TPU:1, one launch (start us, length us, event | category | flops | bytes accessed | tf_op | source)
XLA Modules:
  0.0 200.9 jit_solution(17681774374773401351)
XLA Ops:
  0.0 0.9 copy_bitcast_fusion.1
  0.9 0.6 reduce-window.14
  1.5 0.2 slice_reduce_fusion
  1.7 0.1 broadcast_add_fusion
  1.9 2.0 %copy.32 = f32[16,2,256]{1,2,0:T(8,128)} copy(f32[16,2,256]{2,1,0:T(2,128)S(1)} %reduce_window_sum.30.row_ref) | data formatting | bytes 65536 | tf_op jit(solution)/shard_map/reduce_window_sum
  4.0 0.7 reshape_reshape.3.skip_ref
  4.6 13.2 %shard_map.154 = (f32[256,2048]{1,0:T(8,128)}, f32[128,2048]{1,0:T(8,128)}, f32[1,2048]{1,0:T(1,128)}) custom-call(bf16[256,2048]{1,0:T(8,128)(2,1)} %x_ref.1, f32[16,256,2]{2,1,0:T(8,128)} %bitcast.54, f32[16,2,256]{2,1,0:T(2,128)} %copy-done.8, bf16[256,128]{1,0:T(8,128)(2,1)} %write_ref.1, bf16[256,128]{1,0:T(8,128)(2,1)} %read_ref.3, ...), custom_call_target="tpu_custom_call" | custom-call | tf_op jit(solution)/shard_map/pallas_call | solution.py:376
  17.8 1.2 copy-done.4
  19.1 0.7 copy-done.5
  19.8 12.9 %shard_map.155.prior_ref = bf16[128,2048]{1,0:T(8,128)(2,1)S(1)} custom-call(f32[128,2048]{1,0:T(8,128)S(1)} %copy-done.4, f32[1,2048]{1,0:T(1,128)S(1)} %copy-done.5), custom_call_target="tpu_custom_call" | custom-call | tf_op jit(solution)/shard_map/pallas_call | solution.py:400
  32.7 0.8 copy-done.3
  33.4 4.8 %shard_map.156.normed_ref = bf16[256,2048]{1,0:T(8,128)(2,1)} custom-call(f32[256,2048]{1,0:T(8,128)} %get-tuple-element.8.mixed_ref, bf16[128,2048]{1,0:T(8,128)(2,1)} %copy-done.3, f32[16,256,2]{2,1,0:T(8,128)} %bitcast.55, bf16[256,128]{1,0:T(8,128)(2,1)} %read_ref.3, bf16[256,2048]{1,0:T(8,128)(2,1)} %gate_ref.1, f32[1,2048]{1,0:T(1,128)} %bitcast.63), custom_call_target="tpu_custom_call" | custom-call | tf_op jit(solution)/shard_map/pallas_call | solution.py:415
  38.3 1.2 copy-done.2
  39.5 98.5 %shard_map.157 = f32[256,1024]{1,0:T(8,128)S(1)} custom-call(bf16[256,2048]{1,0:T(8,128)(2,1)S(1)} %copy-done.2, bf16[2048,1024]{1,0:T(8,128)(2,1)} %weight_ref.1), custom_call_target="tpu_custom_call" | custom-call | tf_op jit(solution)/shard_map/pallas_call | solution.py:437
  138.1 1.5 convolution_convert_fusion.1
  139.6 0.2 multiply_reduce_fusion
  139.8 0.1 broadcast_in_dim.46
  140.0 0.6 reduce-window.16
  140.5 0.2 slice_reduce_fusion.1
  140.8 0.1 add_bitcast_fusion
  140.9 0.1 eq.66
  141.0 0.1 fusion.11
  141.1 1.3 convolution_convert_fusion
  142.5 31.2 %shard_map.158 = bf16[4,4,32,256]{3,2,1,0:T(8,128)(2,1)S(1)} custom-call(bf16[4,4,32,384]{3,2,1,0:T(8,128)(2,1)S(1)} %pad_maximum_fusion.src_ref), custom_call_target="tpu_custom_call" | custom-call | tf_op jit(solution)/shard_map/pallas_call | solution.py:348
  173.8 0.9 copy.40
  174.7 1.1 reshape.116
  175.8 3.9 %convolution_convert_fusion.3 = bf16[2,64,1024]{2,1,0:T(8,128)(2,1)} fusion(bf16[2,672,1024]{2,1,0:T(8,128)(2,1)S(1)} %copy-done, bf16[2,64,1024]{2,1,0:T(8,128)(2,1)S(1)} %reshape.116, bf16[2,1024,672]{1,2,0:T(8,128)(2,1)} %param.27), kind=kOutput, calls=%fused_computation.5 | convolution fusion | flops 352710656 | bytes 6029312 | tf_op jit(solution)/shard_map/esf,efl->esl/dot_general | solution.py:519
  179.7 1.1 reshape.117
  180.9 15.5 %shard_map.159 = bf16[4,4,32,256]{3,2,1,0:T(8,128)(2,1)S(1)} custom-call(bf16[4,4,32,256]{3,2,1,0:T(8,128)(2,1)S(1)} %bitcast.52), custom_call_target="tpu_custom_call" | custom-call | tf_op jit(solution)/shard_map/pallas_call | solution.py:348
  196.4 0.2 copy.35
  196.7 0.7 fusion.10
  197.3 3.5 %fusion = bf16[256,1024]{1,0:T(8,128)(2,1)} fusion(bf16[1024,1024]{1,0:T(8,128)(2,1)} %param.29, bf16[256,128]{0,1:T(8,128)(2,1)} %bitcast.62, bf16[128,1024]{1,0:T(8,128)(2,1)S(1)} %bitcast.56, f32[256,1024]{1,0:T(8,128)} %copy-done.1, bf16[256,1024]{1,0:T(8,128)(2,1)S(1)} %copy-done.6), kind=kOutput, calls=%fused_computation.3 | convolution fusion | flops 605290496 | bytes 4521984 | tf_op jit(solution)/shard_map/dot_general | solution.py:525
  (42 shorter events, 0.6 us)
Async XLA Ops:
  0.0 175.8 %copy-start = (bf16[2,672,1024]{2,1,0:T(8,128)(2,1)S(1)}, bf16[2,672,1024]{2,1,0:T(8,128)(2,1)}, u32[]{:S(2)}) copy-start(bf16[2,672,1024]{2,1,0:T(8,128)(2,1)} %param.28) | copy-start | bytes 8257540
  0.0 3.9 %copy-start.13 = (f32[32]{0:T(128)S(1)}, f32[32]{0:T(128)}, u32[]{:S(2)}) copy-start(f32[32]{0:T(128)} %param.20) | copy-start | bytes 388
  1.9 2.8 %copy-start.8 = (f32[16,2,256]{2,1,0:T(2,128)}, f32[16,2,256]{2,1,0:T(2,128)S(1)}, u32[]{:S(2)}) copy-start(f32[16,2,256]{2,1,0:T(2,128)S(1)} %reduce_window_sum.30.row_ref) | copy-start | bytes 98308
  17.8 1.2 copy-start.4
  19.1 0.7 copy-start.5
  32.6 0.8 copy-start.3
  38.3 1.2 copy-start.2
  39.5 98.5 %copy-start.6 = (bf16[256,1024]{1,0:T(8,128)(2,1)S(1)}, bf16[256,1024]{1,0:T(8,128)(2,1)}, u32[]{:S(2)}) copy-start(bf16[256,1024]{1,0:T(8,128)(2,1)} %param.24) | copy-start | bytes 1572868
  39.5 98.5 %copy-start.7 = (bf16[1024,1024]{1,0:T(8,128)(2,1)S(1)}, bf16[1024,1024]{1,0:T(8,128)(2,1)}, u32[]{:S(2)}) copy-start(bf16[1024,1024]{1,0:T(8,128)(2,1)} %param.26) | copy-start | bytes 6291460
  39.5 98.5 %copy-start.12 = (f32[1024]{0:T(1024)S(1)}, f32[1024]{0:T(1024)}, u32[]{:S(2)}) copy-start(f32[1024]{0:T(1024)} %param.25) | copy-start | bytes 12292
  138.0 1.5 copy-start.1
  138.1 1.9 copy-start.9
  180.8 15.8 %copy-start.10 = (s32[256,22]{0,1:T(8,128)S(1)}, s32[256,22]{0,1:T(8,128)}, u32[]{:S(2)}) copy-start(s32[256,22]{0,1:T(8,128)} %param.30) | copy-start | bytes 67588
  180.9 15.8 %copy-start.11 = (s32[256,22]{0,1:T(8,128)S(1)}, s32[256,22]{0,1:T(8,128)}, u32[]{:S(2)}) copy-start(s32[256,22]{0,1:T(8,128)} %param.31) | copy-start | bytes 67588
